TPU v7x, 32 devices: a whole 2x2x4 slice. The times are simulated.
32 devices in a mesh: subj: 16 (over z, y, x), vox: 2 (over core).
Axes of the slice: x: 2, y: 2, z: 4, core: 2. Of those that a mesh axis runs over, the one named last changes fastest.
Arguments:
- bold_series: float32 [16, 300, 16384], P('subj', None, 'vox')
- seed_index: int32 [256], replicated, may hold values from 0 to 16383
Outputs:
- group_z: float32 [16384, 256], P(('vox', 'subj'))
All inputs are finite; a program needn't handle non-finite values.
Results may differ from a plain program's by a relative error of at most 0.00031.
Values may be sent and summed in bfloat16 or wider, within the bound.
A program may use at most 64 MiB of HBM per device.

v0:
```python
import jax
import jax.numpy as jnp
from jax import lax
from jax.sharding import PartitionSpec as P

clip_limit = 0.99
epsilon = 1e-05


def normalize(series):
    demean_series = series - jnp.mean(series, axis=0, keepdims=True)
    spread = jnp.mean(demean_series * demean_series, axis=0, keepdims=True)
    return (demean_series * lax.rsqrt(spread + epsilon)).astype(jnp.bfloat16)


def arctanh_transform(cross_product, length):
    clipped = jnp.clip(cross_product * (1.0 / length), -clip_limit, clip_limit)
    return 0.5 * jnp.log((1.0 + clipped) / (1.0 - clipped))


def correlate(normed, seed_panel):
    return lax.dot_general(
        normed, seed_panel, (((0,), (0,)), ((), ())), preferred_element_type=jnp.float32
    )


def body(bold_series, seed_index):
    length = bold_series.shape[1]
    normed = normalize(bold_series[0])
    columns = normed.shape[1]
    groups = lax.axis_size("subj")
    anchor = lax.axis_index("vox") * columns
    offsets = seed_index - anchor
    inside = (offsets >= 0) & (offsets < columns)
    picked = jnp.take(normed, jnp.clip(offsets, 0, columns - 1), axis=1)
    masked = jnp.where(
        inside[None, :], picked.astype(jnp.float32), jnp.zeros(picked.shape, jnp.float32)
    )
    seed_panel = lax.psum(masked.astype(jnp.bfloat16), "vox")
    summed = lax.psum_scatter(
        arctanh_transform(correlate(normed, seed_panel), length),
        "subj",
        scatter_dimension=0,
        tiled=True,
    )
    return summed * (1.0 / groups)


def solution(mesh):
    in_specs = (P("subj", None, "vox"), P())
    out_specs = P(("vox", "subj"), None)
    return jax.shard_map(body, mesh=mesh, in_specs=in_specs, out_specs=out_specs, check_vma=False)
```

profile of v0, /device:TPU:10, one launch (start us, length us, event | category | flops | bytes accessed | tf_op | source)
XLA Modules:
  0.0 275.5 jit_solution(376455926714964036)
XLA Ops:
  6.5 0.0 all-reduce.2.cloned.1.call-start
  6.5 22.2 %copy.3 = f32[1,300,8192]{1,2,0:T(8,128)} copy(f32[1,300,8192]{2,0,1:T(1,128)} %param.2) | data formatting | bytes 19660800 | tf_op args[0]
  28.7 8.8 %reduce_sum.18 = f32[8192]{0:T(1024)S(1)} reduce(f32[1,300,8192]{2,0,1:T(1,128)} %param.2, f32[]{:T(128)} %constant.14.clone.1), dimensions={0,1}, to_apply=%region_0.0 | reduce | flops 2449408 | bytes 9863172 | tf_op jit(solution)/shard_map/reduce_sum | solution.py:11
  37.6 0.0 copy-start
  37.6 7.0 %multiply_reduce_fusion = f32[8192]{0:T(1024)S(1)} fusion(f32[1,300,8192]{1,2,0:T(8,128)} %copy.3, f32[8192]{0:T(1024)S(1)} %broadcast_multiply_fusion.1), kind=kLoop, calls=%fused_computation.3 | loop fusion | flops 7364608 | bytes 9895936 | tf_op jit(solution)/shard_map/reduce_sum | solution.py:12
  44.6 1.2 copy-done
  45.8 0.0 copy-start.1
  45.9 4.2 %multiply_convert_fusion = bf16[300,8192]{0,1:T(8,128)(2,1)} fusion(f32[1,300,8192]{1,2,0:T(8,128)S(1)} %copy-done, f32[8192]{0:T(1024)S(1)} %add_rsqrt_fusion, f32[8192]{0:T(1024)S(1)} %broadcast_multiply_fusion.1), kind=kLoop, calls=%fused_computation.2 | loop fusion | flops 7372800 | bytes 14811136 | tf_op jit(solution)/shard_map/convert_element_type | solution.py:13
  50.1 0.0 copy-done.1
  50.1 4.7 %gather_fusion = bf16[256,300]{1,0:T(8,128)(2,1)S(1)} fusion(bf16[300,8192]{0,1:T(8,128)(2,1)} %multiply_convert_fusion, s32[1024]{0:T(1024)S(1)} %pad_clamp_fusion), kind=kCustom, calls=%fused_computation | custom fusion | bytes 308224 | tf_op jit(solution)/shard_map/jit(_take)/gather | solution.py:35
  54.8 0.8 fusion.1
  55.7 0.0 all-reduce.2.cloned.1.call-update
  55.7 0.0 reduce-scatter.2.cloned.1.call-start
  55.7 19.6 %all-reduce.2.cloned.1.call-done = bf16[300,256]{0,1:T(8,128)(2,1)} async-done(((bf16[300,256]{0,1:T(8,128)(2,1)}), bf16[300,256]{0,1:T(8,128)(2,1)}) %all-reduce.2.cloned.1.call-update) | async-done | bytes 153616 | tf_op jit(solution)/shard_map/psum | solution.py:39
  75.3 9.3 %log_multiply_fusion = f32[8192,256]{1,0:T(8,128)} fusion(bf16[300,8192]{0,1:T(8,128)(2,1)} %multiply_convert_fusion, bf16[300,256]{0,1:T(8,128)(2,1)} %all-reduce.2.cloned.1.call-done), kind=kOutput, calls=%fused_computation.6 | convolution fusion | flops 1270874112 | bytes 13457408 | tf_op jit(solution)/shard_map/dot_general | solution.py:22
  84.7 0.0 reduce-scatter.2.cloned.1.call-update
  84.7 182.1 %reduce-scatter.2.cloned.1.call-done = f32[512,256]{1,0:T(8,128)} async-done(((f32[8192,256]{1,0:T(8,128)}), f32[512,256]{1,0:T(8,128)}) %reduce-scatter.2.cloned.1.call-update) | async-done | bytes 524304 | tf_op jit(solution)/shard_map/reduce_scatter | solution.py:40
  266.8 1.9 broadcast_multiply_fusion
  (4 shorter events, 0.0 us)
Async XLA Ops:
  6.5 68.8 %all-reduce.2.cloned.1.call-start = ((), (), s32[]{:S(2)}) async-start(), calls=%async_computation.1 | async-start | bytes 393216 | tf_op jit(solution)/shard_map/psum | solution.py:39
  37.6 8.3 %copy-start = (f32[1,300,8192]{1,2,0:T(8,128)S(1)}, f32[1,300,8192]{1,2,0:T(8,128)}, u32[]{:S(2)}) copy-start(f32[1,300,8192]{1,2,0:T(8,128)} %copy.3) | copy-start | bytes 29491204
  45.8 4.2 %copy-start.1 = (s32[256]{0:T(256)S(1)}, s32[256]{0:T(256)}, u32[]{:S(2)}) copy-start(s32[256]{0:T(256)} %param.3) | copy-start | bytes 3076
  55.7 211.1 %reduce-scatter.2.cloned.1.call-start = ((), (), s32[]{:S(2)}) async-start(), calls=%async_computation.2 | async-start | bytes 8912896 | tf_op jit(solution)/shard_map/reduce_scatter | solution.py:40
Sparse Core Ops, SparseCore 0:
  55.8 19.4 all-reduce.1
  84.8 181.9 reduce-scatter.1
where the time goes:
time: 276 us; the launch traced here: 275 us
  waiting for transfers between devices  202 us (73%)
  local copies, waits for them, and re-layouts  28.2 us (10%)
  other arithmetic  22.8 us (8%)
  between operations  13.5 us (5%)
  matrix products  9.32 us (3%)
    reduce_scatter x1, waiting for transfers between devices, body(): lax.psum_scatter(arctanh_transform(correlate(normed, seed_panel), length)...  182 us
    unnamed x5, local copies, waits for them, and re-layouts  23.4 us
    psum x1, waiting for transfers between devices, body(): seed_panel = lax.psum(masked.astype(jnp.bfloat16), 'vox')  19.6 us
    dot_general x1, matrix products, correlate(): lax.dot_general(normed, seed_panel, (((0,), (0,)), ((), ())), preferred_e...  9.32 us
    reduce_sum x1, other arithmetic, normalize(): demean_series = series - jnp.mean(series, axis=0, keepdims=True)  8.82 us
    reduce_sum x1, other arithmetic, normalize(): spread = jnp.mean(demean_series * demean_series, axis=0, keepdims=True)  6.99 us
  transfers between devices with their start and end apart: 2, of which 2 were waited for; matrix products, arithmetic and copies ran while one was open for 0% of the time, Pallas kernels for 0%

commit v1 on v0

--- a/solution.py
+++ b/solution.py
@@ -36,7 +36,9 @@
     masked = jnp.where(
         inside[None, :], picked.astype(jnp.float32), jnp.zeros(picked.shape, jnp.float32)
     )
-    seed_panel = lax.psum(masked.astype(jnp.bfloat16), "vox")
+    x = masked.astype(jnp.bfloat16)
+    parts = lax.all_gather(x, "vox", axis=0, tiled=False)
+    seed_panel = parts.sum(axis=0)
     summed = lax.psum_scatter(
         arctanh_transform(correlate(normed, seed_panel), length),
         "subj",

time: 276 us -> 258 us (0.935)
  waiting for transfers between devices: 202 us -> 182 us
    psum x1 -> x0, waiting for transfers between devices: 19.6 us -> none  [body(): seed_panel = lax.psum(masked.astype(jnp.bfloat16), 'vox')]
  transfers between devices with their start and end apart: 2 -> 1, of which waited for: 2 -> 1; matrix products, arithmetic and copies ran while one was open for 0% -> 0% of each run, Pallas kernels for 0% -> 0%
where the time goes in v1:
time: 258 us; the launch traced here: 257 us
  waiting for transfers between devices  182 us (71%)
  local copies, waits for them, and re-layouts  28.3 us (11%)
  other arithmetic  22 us (9%)
  between operations  13.5 us (5%)
  matrix products  9.1 us (4%)
    reduce_scatter x1, waiting for transfers between devices, body(): lax.psum_scatter(arctanh_transform(correlate(normed, seed_panel), length)...  182 us
    unnamed x5, local copies, waits for them, and re-layouts  23.4 us
    dot_general x1, matrix products, correlate(): lax.dot_general(normed, seed_panel, (((0,), (0,)), ((), ())), preferred_e...  9.1 us
    reduce_sum x1, other arithmetic, normalize(): demean_series = series - jnp.mean(series, axis=0, keepdims=True)  8.82 us
    reduce_sum x1, other arithmetic, normalize(): spread = jnp.mean(demean_series * demean_series, axis=0, keepdims=True)  6.99 us
  transfers between devices with their start and end apart: 1, of which 1 were waited for; matrix products, arithmetic and copies ran while one was open for 0% of the time, Pallas kernels for 0%

profile of v1, /device:TPU:10, one launch (start us, length us, event | category | flops | bytes accessed | tf_op | source)
XLA Modules:
  0.0 257.3 jit_solution(2154392798447492298)
XLA Ops:
  6.5 0.0 reduce-scatter.2.cloned.1.call-start
  6.5 22.2 %copy.7 = f32[1,300,8192]{1,2,0:T(8,128)} copy(f32[1,300,8192]{2,0,1:T(1,128)} %param.2) | data formatting | bytes 19660800 | tf_op args[0]
  28.7 8.8 %reduce_sum.30 = f32[8192]{0:T(1024)S(1)} reduce(f32[1,300,8192]{2,0,1:T(1,128)} %param.2, f32[]{:T(128)} %constant.15.clone.1), dimensions={0,1}, to_apply=%region_0.0 | reduce | flops 2449408 | bytes 9863172 | tf_op jit(solution)/shard_map/reduce_sum | solution.py:11
  37.6 0.0 copy-start
  37.6 7.0 %multiply_reduce_fusion = f32[8192]{0:T(1024)S(1)} fusion(f32[1,300,8192]{1,2,0:T(8,128)} %copy.7, f32[8192]{0:T(1024)S(1)} %broadcast_multiply_fusion.1), kind=kLoop, calls=%fused_computation.3 | loop fusion | flops 7364608 | bytes 9895936 | tf_op jit(solution)/shard_map/reduce_sum | solution.py:12
  44.6 1.2 copy-done
  45.8 0.0 copy-start.1
  45.9 4.2 %multiply_convert_fusion = bf16[300,8192]{0,1:T(8,128)(2,1)} fusion(f32[1,300,8192]{1,2,0:T(8,128)S(1)} %copy-done, f32[8192]{0:T(1024)S(1)} %add_rsqrt_fusion, f32[8192]{0:T(1024)S(1)} %broadcast_multiply_fusion.1), kind=kLoop, calls=%fused_computation.2 | loop fusion | flops 7372800 | bytes 14811136 | tf_op jit(solution)/shard_map/convert_element_type | solution.py:13
  50.1 0.0 copy-done.1
  50.1 4.7 %gather_fusion = bf16[256,300]{1,0:T(8,128)(2,1)S(1)} fusion(bf16[300,8192]{0,1:T(8,128)(2,1)} %multiply_convert_fusion, s32[1024]{0:T(1024)S(1)} %pad_clamp_fusion), kind=kCustom, calls=%fused_computation | custom fusion | bytes 308224 | tf_op jit(solution)/shard_map/jit(_take)/gather | solution.py:35
  54.8 0.1 copy.8
  55.0 2.0 all_gather.4
  57.1 0.1 reduce_sum.32
  57.1 9.1 %log_multiply_fusion = f32[8192,256]{1,0:T(8,128)} fusion(bf16[300,8192]{0,1:T(8,128)(2,1)} %multiply_convert_fusion, bf16[300,256]{1,0:T(8,128)(2,1)S(1)} %reduce_sum.32), kind=kOutput, calls=%fused_computation.6 | convolution fusion | flops 1270874112 | bytes 13457408 | tf_op jit(solution)/shard_map/dot_general | solution.py:22
  66.2 0.0 reduce-scatter.2.cloned.1.call-update
  66.2 182.3 %reduce-scatter.2.cloned.1.call-done = f32[512,256]{1,0:T(8,128)} async-done(((f32[8192,256]{1,0:T(8,128)}), f32[512,256]{1,0:T(8,128)}) %reduce-scatter.2.cloned.1.call-update) | async-done | bytes 524304 | tf_op jit(solution)/shard_map/reduce_scatter | solution.py:42
  248.5 1.9 broadcast_multiply_fusion
  (5 shorter events, 0.1 us)
Async XLA Ops:
  6.5 242.0 %reduce-scatter.2.cloned.1.call-start = ((), (), s32[]{:S(2)}) async-start(), calls=%async_computation.1 | async-start | bytes 8912896 | tf_op jit(solution)/shard_map/reduce_scatter | solution.py:42
  37.6 8.3 %copy-start = (f32[1,300,8192]{1,2,0:T(8,128)S(1)}, f32[1,300,8192]{1,2,0:T(8,128)}, u32[]{:S(2)}) copy-start(f32[1,300,8192]{1,2,0:T(8,128)} %copy.7) | copy-start | bytes 29491204
  45.8 4.2 %copy-start.1 = (s32[256]{0:T(256)S(1)}, s32[256]{0:T(256)}, u32[]{:S(2)}) copy-start(s32[256]{0:T(256)} %param.3) | copy-start | bytes 3076
Sparse Core Ops, SparseCore 0:
  66.4 182.1 reduce-scatter.1
